TPU v7x, 32 devices: a whole 2x2x4 slice. The times are simulated.
32 devices in a mesh: dp: 4 (over y, x), tensor: 8 (over z, core).
Axes of the slice: x: 2, y: 2, z: 4, core: 2. Of those that a mesh axis runs over, the one named last changes fastest.
Arguments:
- noisy: bfloat16 [32, 256, 1152], P('dp', None, 'tensor'), may hold values from -6 to 6
- labels: int32 [32], P('dp'), may hold values from 0 to 999
- tsteps: int32 [32], P('dp'), may hold values from 0 to 999
- guide_index: int32 [32], P('dp'), may hold values from 0 to 31
- class_table: bfloat16 [1001, 1152], replicated, may hold values from -6 to 6
- time_table: bfloat16 [1000, 1152], replicated, may hold values from -6 to 6
- guide_table: bfloat16 [32, 1152], replicated, may hold values from -6 to 6
- guide_weights: float32 [32], replicated, may hold values from 0.5 to 4
- teacher_qkv: bfloat16 [1152, 3456], P(None, 'tensor'), may hold values from -0.1875 to 0.1875
- teacher_out: bfloat16 [1152, 1152], P('tensor'), may hold values from -0.1875 to 0.1875
- teacher_ada: bfloat16 [3, 1152, 1152], P(None, None, 'tensor'), may hold values from -0.1875 to 0.1875
- student_qkv: bfloat16 [1152, 3456], P(None, 'tensor'), may hold values from -0.1875 to 0.1875
- student_out: bfloat16 [1152, 1152], P('tensor'), may hold values from -0.1875 to 0.1875
- student_ada: bfloat16 [3, 1152, 1152], P(None, None, 'tensor'), may hold values from -0.1875 to 0.1875
Outputs:
- grad_qkv: float32 [1152, 3456], P('dp', 'tensor')
- grad_out: float32 [1152, 1152], P('tensor', 'dp')
- grad_ada: float32 [3, 1152, 1152], P(None, 'dp', 'tensor')
All inputs are finite; a program needn't handle non-finite values.
Results may differ from a plain program's by a relative error of at most 0.034.
Values may be sent and summed in bfloat16 or wider, within the bound.
A program may use at most 128 MiB of HBM per device.

v0:
```python
import math
import jax
import jax.numpy as jnp
from jax import lax
from jax.sharding import PartitionSpec as P

HD = 72
norm_eps = 1e-06


def lookup_rows(indices, table_rows):
    one_hot = (
        indices[:, None] == jnp.arange(table_rows.shape[0], dtype=jnp.int32)[None, :]
    ).astype(table_rows.dtype)
    return jnp.dot(one_hot, table_rows, preferred_element_type=jnp.float32)


def attend(qkv_sums, heads_here):
    batch_rows, seq_len = (qkv_sums.shape[0], qkv_sums.shape[1])
    heads_qkv = qkv_sums.astype(jnp.bfloat16).reshape(batch_rows, seq_len, heads_here, 3, HD)
    queries, key_rows, values = (
        heads_qkv[:, :, :, 0],
        heads_qkv[:, :, :, 1],
        heads_qkv[:, :, :, 2],
    )
    scores = jnp.einsum(
        "blhe,bmhe->bhlm", queries, key_rows, preferred_element_type=jnp.float32
    ) * (1.0 / math.sqrt(HD))
    exponent = jnp.exp(scores - jnp.max(scores, axis=-1, keepdims=True))
    attn_prob = exponent / jnp.sum(exponent, axis=-1, keepdims=True)
    prob_low = attn_prob.astype(jnp.bfloat16)
    attn_mixed = jnp.einsum("bhlm,bmhe->blhe", prob_low, values, preferred_element_type=jnp.float32)
    attn_mixed = attn_mixed.astype(jnp.bfloat16).reshape(batch_rows, seq_len, heads_here * HD)
    return (heads_qkv, attn_prob, prob_low, attn_mixed)


def attend_grad(heads_qkv, attn_prob, prob_low, grad_low):
    batch_rows, seq_len = (heads_qkv.shape[0], heads_qkv.shape[1])
    queries, key_rows, values = (
        heads_qkv[:, :, :, 0],
        heads_qkv[:, :, :, 1],
        heads_qkv[:, :, :, 2],
    )
    grad_probs = jnp.einsum("blhe,bmhe->bhlm", grad_low, values, preferred_element_type=jnp.float32)
    row_delta = jnp.sum(attn_prob * grad_probs, axis=-1, keepdims=True)
    grad_scores = (attn_prob * (grad_probs - row_delta) * (1.0 / math.sqrt(HD))).astype(
        jnp.bfloat16
    )
    grad_query = jnp.einsum(
        "bhlm,bmhe->blhe", grad_scores, key_rows, preferred_element_type=jnp.float32
    )
    grad_keys = jnp.einsum(
        "bhlm,blhe->bmhe", grad_scores, queries, preferred_element_type=jnp.float32
    )
    grad_values = jnp.einsum(
        "bhlm,blhe->bmhe", prob_low, grad_low, preferred_element_type=jnp.float32
    )
    grad_qkv_act = jnp.stack([grad_query, grad_keys, grad_values], axis=3).astype(jnp.bfloat16)
    return grad_qkv_act.reshape(batch_rows, seq_len, -1)


def forward(source, embed_act, qkv_weight, out_weight, ada_weight):
    heads_here = out_weight.shape[0] // HD
    modulation = jnp.einsum(
        "bd,kde->bke", embed_act, ada_weight, preferred_element_type=jnp.float32
    )
    wide_mod = lax.all_gather(modulation, "tensor", axis=2, tiled=True)
    full_rows = (
        source.astype(jnp.float32) * (1.0 + wide_mod[:, 1][:, None]) + wide_mod[:, 0][:, None]
    ).astype(jnp.bfloat16)
    qkv_sums = jnp.einsum("bld,df->blf", full_rows, qkv_weight, preferred_element_type=jnp.float32)
    heads_qkv, attn_prob, prob_low, attn_mixed = attend(qkv_sums, heads_here)
    partial_value = jnp.einsum(
        "blf,fd->bld", attn_mixed, out_weight, preferred_element_type=jnp.float32
    )
    projected = lax.psum_scatter(
        partial_value.astype(jnp.bfloat16), "tensor", scatter_dimension=2, tiled=True
    ).astype(jnp.float32)
    branch = modulation[:, 2][:, None] * projected
    return (branch, (full_rows, heads_qkv, attn_prob, prob_low, attn_mixed, projected, modulation))


def local(
    noisy,
    labels,
    tsteps,
    guide_index,
    class_table,
    time_table,
    guide_table,
    guide_weights,
    teacher_qkv,
    teacher_out,
    teacher_ada,
    student_qkv,
    student_out,
    student_ada,
):
    samples, seq_len, width_part = noisy.shape
    model_width = width_part * lax.axis_size("tensor")
    batch_size = samples * lax.axis_size("dp")
    signal = noisy.astype(jnp.float32)
    row_sums = lax.psum((jnp.sum(signal, axis=2), jnp.sum(signal * signal, axis=2)), "tensor")
    row_mean = row_sums[0] / model_width
    row_var = row_sums[1] / model_width - row_mean * row_mean
    normed = ((signal - row_mean[:, :, None]) * lax.rsqrt(row_var + norm_eps)[:, :, None]).astype(
        jnp.bfloat16
    )
    null_class = class_table.shape[0] - 1
    time_embed = lookup_rows(tsteps, time_table)
    cond_embed = lookup_rows(labels, class_table) + time_embed
    null_embed = class_table[null_class].astype(jnp.float32)[None, :] + time_embed
    guide_hot = guide_index[:, None] == jnp.arange(guide_table.shape[0], dtype=jnp.int32)[None, :]
    student_embed = cond_embed + jnp.dot(
        guide_hot.astype(jnp.bfloat16), guide_table, preferred_element_type=jnp.float32
    )
    strength = jnp.sum(jnp.where(guide_hot, guide_weights[None, :], 0.0), axis=1)
    cond_act = jax.nn.silu(cond_embed).astype(jnp.bfloat16)
    null_act = jax.nn.silu(null_embed).astype(jnp.bfloat16)
    student_act = jax.nn.silu(student_embed).astype(jnp.bfloat16)
    scale_norm = 1.0 / math.sqrt(batch_size * seq_len)
    wide_rows = lax.all_gather(normed, "tensor", axis=2, tiled=True)
    teacher_full = jnp.concatenate([wide_rows, wide_rows], axis=0)
    teacher_act = jnp.concatenate([cond_act, null_act], axis=0)
    teacher_branch, unused_saved = forward(
        teacher_full, teacher_act, teacher_qkv, teacher_out, teacher_ada
    )
    teacher_update = teacher_branch.astype(jnp.bfloat16).astype(jnp.float32)
    scaled = strength[:, None, None]
    target = signal + (
        (1.0 + scaled) * teacher_update[:samples] - scaled * teacher_update[samples:]
    )
    branch, saved = forward(wide_rows, student_act, student_qkv, student_out, student_ada)
    full_rows, heads_qkv, attn_prob, prob_low, attn_mixed, projected, modulation = saved
    heads_here = student_out.shape[0] // HD
    cotangent = (signal + branch - target) * scale_norm
    grad_gate = jnp.sum(cotangent * projected, axis=1)
    grad_proj = (cotangent * modulation[:, 2][:, None]).astype(jnp.bfloat16)
    gathered = lax.all_gather(grad_proj, "tensor", axis=2, tiled=True)
    grad_mixed = jnp.einsum(
        "bld,ed->ble", gathered, student_out, preferred_element_type=jnp.float32
    )
    block_grad = jnp.einsum("ble,bld->ed", attn_mixed, gathered, preferred_element_type=jnp.float32)
    grad_mixed, grad_out_rows = (grad_mixed, block_grad)
    grad_low = grad_mixed.astype(jnp.bfloat16).reshape(samples, seq_len, heads_here, HD)
    grad_qkv_act = attend_grad(heads_qkv, attn_prob, prob_low, grad_low)
    grad_qkv_local = jnp.einsum(
        "bld,blf->df", full_rows, grad_qkv_act, preferred_element_type=jnp.float32
    )
    input_terms = jnp.einsum(
        "blf,df->bld", grad_qkv_act, student_qkv, preferred_element_type=jnp.float32
    )
    grad_input = lax.psum_scatter(
        input_terms.astype(jnp.bfloat16), "tensor", scatter_dimension=2, tiled=True
    ).astype(jnp.float32)
    grad_shift = jnp.sum(grad_input, axis=1)
    grad_scale = jnp.sum(grad_input * normed.astype(jnp.float32), axis=1)
    grad_modulation = jnp.stack([grad_shift, grad_scale, grad_gate], axis=1)
    grad_ada_local = jnp.einsum(
        "bd,bke->kde",
        student_act.astype(jnp.float32),
        grad_modulation,
        precision=lax.Precision.HIGHEST,
    )
    grad_qkv, grad_out, grad_ada = (
        lax.psum_scatter(
            grad_qkv_local.astype(jnp.bfloat16), "dp", scatter_dimension=0, tiled=True
        ).astype(jnp.float32),
        lax.psum_scatter(
            grad_out_rows.astype(jnp.bfloat16), "dp", scatter_dimension=1, tiled=True
        ).astype(jnp.float32),
        lax.psum_scatter(
            grad_ada_local.astype(jnp.bfloat16), "dp", scatter_dimension=1, tiled=True
        ).astype(jnp.float32),
    )
    return (grad_qkv, grad_out, grad_ada)


def solution(mesh):
    return jax.shard_map(
        local,
        mesh=mesh,
        in_specs=(
            P("dp", None, "tensor"),
            P("dp"),
            P("dp"),
            P("dp"),
            P(),
            P(),
            P(),
            P(),
            P(None, "tensor"),
            P("tensor", None),
            P(None, None, "tensor"),
            P(None, "tensor"),
            P("tensor", None),
            P(None, None, "tensor"),
        ),
        out_specs=(P("dp", "tensor"), P("tensor", "dp"), P(None, "dp", "tensor")),
        check_vma=False,
    )
```

profile of v0, /device:TPU:0, one launch (start us, length us, event | category | flops | bytes accessed | tf_op | source)
XLA Modules:
  0.0 544.9 jit_solution(2838430340158237559)
XLA Ops:
  7.2 1.4 convert_reduce_fusion
  8.6 30.3 %all-reduce = (f32[8,256]{1,0:T(8,128)S(1)}, f32[8,256]{1,0:T(8,128)S(1)}) all-reduce(f32[8,256]{1,0:T(8,128)S(1)} %get-tuple-element.6, f32[8,256]{1,0:T(8,128)S(1)} %get-tuple-element.5), channel_id=1, replica_groups=mesh['dp'=4,'tensor'=8] {'tensor'}, use_global_device_ids=true, to_apply=%region_3.0 | all-reduce | flops 4096 | bytes 32768 | tf_op jit(solution)/shard_map/psum | solution.py:103
  38.9 2.0 fusion.54
  41.8 1.1 multiply_convert_fusion.3
  42.9 2.1 multiply_convert_fusion.4
  45.7 40.4 %all_gather.14 = f32[16,3,1152]{0,1,2:T(4,128)S(1)} all-gather(f32[16,3,144]{0,1,2:T(4,128)S(1)} %copy.72), channel_id=1, replica_groups=mesh['dp'=4,'tensor'=8] {'tensor'}, dimensions={2}, use_global_device_ids=true | all-gather | bytes 248832 | tf_op jit(solution)/shard_map/all_gather | solution.py:67
  86.1 0.9 slice_add_fusion
  87.4 18.4 %all-gather.3.cloned.1.call-done = bf16[8,256,1152]{1,2,0:T(8,128)(2,1)} async-done(((bf16[8,256,144]{1,2,0:T(8,128)(2,1)}), bf16[8,256,1152]{1,2,0:T(8,128)(2,1)}) %all-gather.3.cloned.1.call-update) | async-done | bytes 4718608 | tf_op jit(solution)/shard_map/all_gather | solution.py:122
  105.8 10.8 %fusion.31 = bf16[16,256,432]{1,2,0:T(8,128)(2,1)S(1)} fusion(bf16[8,256,1152]{1,2,0:T(8,128)(2,1)} %all-gather.3.cloned.1.call-done, f32[16,1152]{1,0:T(8,128)S(1)} %copy.74, f32[16,1152]{1,0:T(8,128)S(1)} %copy.73, bf16[1152,432]{0,1:T(8,128)(2,1)} %param.22), kind=kOutput, calls=%fused_computation.35 | convolution fusion | flops 4111663104 | bytes 9400320 | tf_op jit(solution)/shard_map/bld,df->blf/dot_general | solution.py:71
  116.6 1.7 copy-done.7
  118.4 1.3 fusion.59
  119.7 6.3 %fusion.94 = (f32[16,2,256]{2,1,0:T(2,128)S(1)}, f32[16,2,256,256]{2,3,1,0:T(8,128)S(1)}) fusion(f32[16,2,256,256]{2,3,1,0:T(8,128)S(1)} %fusion.59), kind=kOutput, calls=%fused_computation.132 | output fusion | flops 8388863 | bytes 16809984 | tf_op jit(solution)/shard_map/sub | solution.py:29
  126.0 2.3 fusion.37
  128.3 5.3 convolution_convert_fusion
  133.7 0.8 copy-done.15
  135.5 42.4 %all_gather.13 = f32[8,3,1152]{0,1,2:T(4,128)S(1)} all-gather(f32[8,3,144]{0,1,2:T(4,128)S(1)} %copy.64), channel_id=1, replica_groups=mesh['dp'=4,'tensor'=8] {'tensor'}, dimensions={2}, use_global_device_ids=true | all-gather | bytes 124416 | tf_op jit(solution)/shard_map/all_gather | solution.py:67
  177.9 0.9 slice_add_fusion.1
  179.3 5.9 %fusion.36 = bf16[8,256,432]{1,2,0:T(8,128)(2,1)S(1)} fusion(bf16[8,256,1152]{1,2,0:T(8,128)(2,1)} %all-gather.3.cloned.1.call-done, f32[8,1152]{1,0:T(8,128)S(1)} %copy.66, f32[8,1152]{1,0:T(8,128)S(1)} %copy.65, bf16[1152,432]{0,1:T(8,128)(2,1)S(1)} %copy-done.13), kind=kOutput, calls=%fused_computation.50 | convolution fusion | flops 2048753664 | bytes 7557120 | tf_op jit(solution)/shard_map/bld,df->blf/dot_general | solution.py:71
  185.9 3.2 fusion.93
  189.7 1.5 copy-done.3
  191.2 3.6 convolution_convert_fusion.2
  195.1 54.8 %reduce-scatter.13.cloned.1.call-done = bf16[16,256,144]{1,2,0:T(8,128)(2,1)} async-done(((bf16[16,256,1152]{1,2,0:T(8,128)(2,1)}), bf16[16,256,144]{1,2,0:T(8,128)(2,1)}) %reduce-scatter.13.cloned.1.call-update) | async-done | bytes 1179664 | tf_op jit(solution)/shard_map/reduce_scatter | solution.py:76
  249.9 3.1 fusion.57
  253.0 54.6 %reduce-scatter.11.cloned.1.call-done = bf16[8,256,144]{1,2,0:T(8,128)(2,1)} async-done(((bf16[8,256,1152]{1,2,0:T(8,128)(2,1)}), bf16[8,256,144]{1,2,0:T(8,128)(2,1)}) %reduce-scatter.11.cloned.1.call-update) | async-done | bytes 589840 | tf_op jit(solution)/shard_map/reduce_scatter | solution.py:76
  307.6 2.7 fusion.51
  310.3 1.0 multiply_convert_fusion.2
  311.6 49.6 %all-gather.5.cloned.1.call-done = bf16[8,256,1152]{1,2,0:T(8,128)(2,1)} async-done(((bf16[8,256,144]{1,2,0:T(8,128)(2,1)}), bf16[8,256,1152]{1,2,0:T(8,128)(2,1)}) %all-gather.5.cloned.1.call-update) | async-done | bytes 4718608 | tf_op jit(solution)/shard_map/all_gather | solution.py:139
  361.2 3.4 convolution_convert_fusion.4
  365.6 3.8 fusion.66
  369.4 7.7 %fusion.48 = bf16[8,256,2,1,72]{1,4,2,0,3:T(8,128)(2,1)S(1)} fusion(f32[8,2,256,256]{2,3,1,0:T(8,128)} %fusion.66, bf16[8,256,2,3,72]{1,4,3,2,0:T(8,128)(2,1)} %bitcast.136, f32[8,2,256,256]{2,3,1,0:T(8,128)} %copy-done.3, f32[8,2,256]{2,1,0:T(2,128)S(1)} %get-tuple-element.17), kind=kOutput, calls=%fused_computation.63 | convolution fusion | flops 158634240 | bytes 17989632 | tf_op jit(solution)/shard_map/bhlm,bmhe->blhe/dot_general | solution.py:49
  377.1 7.6 %fusion.45 = bf16[8,256,2,1,72]{1,4,2,0,3:T(8,128)(2,1)S(1)} fusion(f32[8,2,256,256]{2,3,1,0:T(8,128)} %fusion.66, bf16[8,256,2,3,72]{1,4,3,2,0:T(8,128)(2,1)} %bitcast.137, f32[8,2,256,256]{2,3,1,0:T(8,128)} %copy-done.3, f32[8,2,256]{2,1,0:T(2,128)S(1)} %get-tuple-element.17), kind=kOutput, calls=%fused_computation.62 | convolution fusion | flops 158634240 | bytes 17989632 | tf_op jit(solution)/shard_map/bhlm,blhe->bmhe/dot_general | solution.py:52
  385.1 1.2 copy-done.5
  386.3 4.4 convolution_convert_fusion.1
  390.8 4.0 fusion.32
  394.7 1.1 copy.91
  395.9 6.4 %fusion.23 = bf16[1152,432]{1,0:T(8,128)(2,1)} fusion(bf16[8,256,432]{1,2,0:T(8,128)(2,1)} %bitcast.132, bf16[8,256,1152]{1,2,0:T(8,128)(2,1)} %all-gather.3.cloned.1.call-done, f32[8,1152]{1,0:T(8,128)S(1)} %copy.66, f32[8,1152]{1,0:T(8,128)S(1)} %copy.65), kind=kOutput, calls=%fused_computation.29 | convolution fusion | flops 2048366592 | bytes 7557120 | tf_op jit(solution)/shard_map/bld,blf->df/dot_general | solution.py:147
  402.6 41.9 %reduce-scatter.17.cloned.1.call-done = bf16[8,256,144]{1,2,0:T(8,128)(2,1)} async-done(((bf16[8,256,1152]{1,2,0:T(8,128)(2,1)}), bf16[8,256,144]{1,2,0:T(8,128)(2,1)}) %reduce-scatter.17.cloned.1.call-update) | async-done | bytes 589840 | tf_op jit(solution)/shard_map/reduce_scatter | solution.py:153
  444.5 1.7 convert_reduce_fusion.1
  446.2 1.0 fusion.24
  447.2 3.2 copy.93
  450.5 5.6 %reshape.56 = bf16[1152,432]{1,0:T(8,128)(2,1)} reshape(bf16[1152,3,144]{2,1,0:T(4,128)(2,1)} %bitcast.120) | data formatting | bytes 1990656
  456.0 15.7 %reduce-scatter.19.cloned.1.call-done = bf16[288,144]{1,0:T(8,128)(2,1)} async-done(((bf16[1152,144]{1,0:T(8,128)(2,1)}), bf16[288,144]{1,0:T(8,128)(2,1)}) %reduce-scatter.19.cloned.1.call-update) | async-done | bytes 82960
  471.7 1.0 copy.92
  473.5 29.9 %reduce-scatter.15.cloned.1.call-done = bf16[288,432]{1,0:T(8,128)(2,1)} async-done(((bf16[1152,432]{1,0:T(8,128)(2,1)}), bf16[288,432]{1,0:T(8,128)(2,1)}) %reduce-scatter.15.cloned.1.call-update) | async-done | bytes 248848 | tf_op jit(solution)/shard_map/reduce_scatter | solution.py:166
  503.4 1.8 convert_element_type.147
  505.2 29.8 %reduce-scatter.21.cloned.1.call-done = bf16[288,432]{1,0:T(8,128)(2,1)} async-done(((bf16[1152,432]{1,0:T(8,128)(2,1)}), bf16[288,432]{1,0:T(8,128)(2,1)}) %reduce-scatter.21.cloned.1.call-update) | async-done | bytes 248848
  535.0 1.8 reshape.57
  537.2 0.9 convert_element_type.155
  (71 shorter events, 7.9 us)
Async XLA Ops:
  7.2 34.6 %copy-start = (bf16[1000,1152]{1,0:T(8,128)(2,1)S(1)}, bf16[1000,1152]{1,0:T(8,128)(2,1)}, u32[]{:S(2)}) copy-start(bf16[1000,1152]{1,0:T(8,128)(2,1)} %param.19) | copy-start | bytes 6912004
  7.2 35.7 %copy-start.12 = (s32[8]{0:T(128)S(1)}, s32[8]{0:T(128)}, u32[]{:S(2)}) copy-start(s32[8]{0:T(128)} %param.15) | copy-start | bytes 100
  7.2 37.9 %copy-start.9 = (bf16[3,1152,144]{1,2,0:T(8,128)(2,1)S(1)}, bf16[3,1152,144]{1,2,0:T(8,128)(2,1)}, u32[]{:S(2)}) copy-start(bf16[3,1152,144]{1,2,0:T(8,128)(2,1)} %param.24) | copy-start | bytes 2985988
  7.2 98.6 %all-gather.3.cloned.1.call-start = ((), (), s32[]{:S(2)}) async-start(), calls=%async_computation.6 | async-start | bytes 5308416 | tf_op jit(solution)/shard_map/all_gather | solution.py:122
  41.0 208.9 %reduce-scatter.13.cloned.1.call-start = ((), (), s32[]{:S(2)}) async-start(), calls=%async_computation.8 | async-start | bytes 10616832 | tf_op jit(solution)/shard_map/reduce_scatter | solution.py:76
  116.6 1.8 copy-start.7
  126.0 2.3 copy-start.11
  133.6 0.9 copy-start.15
  133.6 0.9 copy-start.16
  133.6 1.3 copy-start.10
  133.7 45.6 %copy-start.13 = (bf16[1152,432]{0,1:T(8,128)(2,1)S(1)}, bf16[1152,432]{0,1:T(8,128)(2,1)}, u32[]{:S(2)}) copy-start(bf16[1152,432]{0,1:T(8,128)(2,1)} %param.25) | copy-start | bytes 2985988
  133.7 173.9 %reduce-scatter.11.cloned.1.call-start = ((), (), s32[]{:S(2)}) async-start(), calls=%async_computation.7 | async-start | bytes 5308416 | tf_op jit(solution)/shard_map/reduce_scatter | solution.py:76
  185.2 4.0 copy-start.6
  189.2 2.0 copy-start.3
  189.2 2.0 copy-start.8
  191.2 3.7 copy-start.17
  194.8 112.8 %copy-start.2 = (bf16[8,256,144]{1,2,0:T(8,128)(2,1)S(1)}, bf16[8,256,144]{1,2,0:T(8,128)(2,1)}, u32[]{:S(2)}) copy-start(bf16[8,256,144]{1,2,0:T(8,128)(2,1)} %param.14) | copy-start | bytes 1769476
  194.9 166.3 %all-gather.5.cloned.1.call-start = ((), (), s32[]{:S(2)}) async-start(), calls=%async_computation.9 | async-start | bytes 5308416 | tf_op jit(solution)/shard_map/all_gather | solution.py:139
  311.3 133.2 %reduce-scatter.17.cloned.1.call-start = ((), (), s32[]{:S(2)}) async-start(), calls=%async_computation.11 | async-start | bytes 5308416 | tf_op jit(solution)/shard_map/reduce_scatter | solution.py:153
  361.2 3.6 copy-start.4
  384.7 1.5 copy-start.14
  385.1 1.2 copy-start.5
  390.7 81.0 %reduce-scatter.19.cloned.1.call-start = ((), (), s32[]{:S(2)}) async-start(), calls=%async_computation.12 | async-start | bytes 737280
  395.8 107.5 %reduce-scatter.15.cloned.1.call-start = ((), (), s32[]{:S(2)}) async-start(), calls=%async_computation.10 | async-start | bytes 1474560 | tf_op jit(solution)/shard_map/reduce_scatter | solution.py:166
  402.3 132.7 %reduce-scatter.21.cloned.1.call-start = ((), (), s32[]{:S(2)}) async-start(), calls=%async_computation.13 | async-start | bytes 1474560
  450.5 87.6 %copy-start.1 = (bf16[1000,1152]{1,0:T(8,128)(2,1)S(1)}, bf16[1000,1152]{1,0:T(8,128)(2,1)}, u32[]{:S(2)}) copy-start(bf16[1000,1152]{1,0:T(8,128)(2,1)} %param.19) | copy-start | bytes 6912004
Sparse Core Ops, SparseCore 0:
  41.1 64.6 all-gather.2
  133.8 116.0 reduce-scatter.12
  252.2 55.3 reduce-scatter.10
  311.5 49.6 all-gather.4
  390.9 53.6 reduce-scatter.16
  447.8 23.8 reduce-scatter.18
  474.6 28.6 reduce-scatter.14
  506.3 28.6 reduce-scatter.20
where the time goes:
time: 546 us; the launch traced here: 545 us
  waiting for transfers between devices  295 us (54%)
  blocking collectives  113 us (21%)
  matrix products  73.9 us (14%)
  other arithmetic  27.9 us (5%)
  local copies, waits for them, and re-layouts  19.9 us (4%)
  between operations  14.5 us (3%)
    reduce_scatter x2, waiting for transfers between devices, forward(): lax.psum_scatter(partial_value.astype(jnp.bfloat16), 'tensor', scatter_di...  109 us
    all_gather x2, blocking collectives, forward(): wide_mod = lax.all_gather(modulation, 'tensor', axis=2, tiled=True)  82.8 us
    all_gather x1, waiting for transfers between devices, local(): gathered = lax.all_gather(grad_proj, 'tensor', axis=2, tiled=True)  49.6 us
    unnamed x10, waiting for transfers between devices  45.6 us
    reduce_scatter x1, waiting for transfers between devices, local(): lax.psum_scatter(input_terms.astype(jnp.bfloat16), 'tensor', scatter_dime...  41.9 us
    psum x1, blocking collectives, local(): lax.psum((jnp.sum(signal, axis=2), jnp.sum(signal * signal, axis=2)), 'te...  30.3 us
    reduce_scatter x1, waiting for transfers between devices, local(): lax.psum_scatter(grad_qkv_local.astype(jnp.bfloat16), 'dp', scatter_dimen...  29.9 us
    unnamed x42, local copies, waits for them, and re-layouts  18.7 us
  transfers between devices with their start and end apart: 8, of which 8 were waited for; matrix products, arithmetic and copies ran while one was open for 10% of the time, Pallas kernels for 0%

commit v1 on v0

--- a/solution.py
+++ b/solution.py
@@ -64,7 +64,14 @@
     modulation = jnp.einsum(
         "bd,kde->bke", embed_act, ada_weight, preferred_element_type=jnp.float32
     )
-    wide_mod = lax.all_gather(modulation, "tensor", axis=2, tiled=True)
+    peers = lax.axis_size("tensor")
+    right = [(i, (i + 1) % peers) for i in range(peers)]
+    blocks = [modulation]
+    for far in range(1, peers):
+        blocks = [lax.ppermute(blocks[0], "tensor", right), *blocks]
+    result = jnp.concatenate(blocks, axis=2)
+    shift = (lax.axis_index("tensor") + 1) * blocks[-1].shape[2]
+    wide_mod = jnp.roll(result, shift, axis=2)
     full_rows = (
         source.astype(jnp.float32) * (1.0 + wide_mod[:, 1][:, None]) + wide_mod[:, 0][:, None]
     ).astype(jnp.bfloat16)

time: 546 us -> 517 us (0.947)
  blocking collectives: 113 us -> 30.3 us
  waiting for transfers between devices: 295 us -> 349 us
    ppermute x0 -> x14, waiting for transfers between devices: none -> 83.4 us  [forward(): blocks = [lax.ppermute(blocks[0], 'tensor', right), *blocks]]
    all_gather x2 -> x0, blocking collectives: 82.8 us -> none  [forward(): wide_mod = lax.all_gather(modulation, 'tensor', axis=2, tiled=True)]
    all_gather x1, waiting for transfers between devices: 18.4 us -> 3.35 us  [local(): wide_rows = lax.all_gather(normed, 'tensor', axis=2, tiled=True)]
    reduce_scatter x2, waiting for transfers between devices: 109 us -> 95.1 us  [forward(): lax.psum_scatter(partial_value.astype(jnp.bfloat16), 'tensor', scatter_di...]
  transfers between devices with their start and end apart: 8 -> 22, of which waited for: 8 -> 22; matrix products, arithmetic and copies ran while one was open for 10% -> 10% of each run, Pallas kernels for 0% -> 0%
where the time goes in v1:
time: 517 us; the launch traced here: 516 us
  waiting for transfers between devices  349 us (68%)
  matrix products  76 us (15%)
  blocking collectives  30.3 us (6%)
  other arithmetic  26.2 us (5%)
  local copies, waits for them, and re-layouts  19 us (4%)
  between operations  14.5 us (3%)
    reduce_scatter x2, waiting for transfers between devices, forward(): lax.psum_scatter(partial_value.astype(jnp.bfloat16), 'tensor', scatter_di...  95.1 us
    ppermute x14, waiting for transfers between devices, forward(): blocks = [lax.ppermute(blocks[0], 'tensor', right), *blocks]  83.4 us
    all_gather x1, waiting for transfers between devices, local(): gathered = lax.all_gather(grad_proj, 'tensor', axis=2, tiled=True)  49.8 us
    unnamed x10, waiting for transfers between devices  45.7 us
    reduce_scatter x1, waiting for transfers between devices, local(): lax.psum_scatter(input_terms.astype(jnp.bfloat16), 'tensor', scatter_dime...  42 us
    psum x1, blocking collectives, local(): lax.psum((jnp.sum(signal, axis=2), jnp.sum(signal * signal, axis=2)), 'te...  30.3 us
    reduce_scatter x1, waiting for transfers between devices, local(): lax.psum_scatter(grad_qkv_local.astype(jnp.bfloat16), 'dp', scatter_dimen...  29.9 us
    unnamed x42, local copies, waits for them, and re-layouts  18.4 us
  transfers between devices with their start and end apart: 22, of which 22 were waited for; matrix products, arithmetic and copies ran while one was open for 10% of the time, Pallas kernels for 0%

profile of v1, /device:TPU:0, one launch (start us, length us, event | category | flops | bytes accessed | tf_op | source)
XLA Modules:
  0.0 516.2 jit_solution(6401181193630638002)
XLA Ops:
  8.6 30.3 %all-reduce = (f32[8,256]{1,0:T(8,128)S(1)}, f32[8,256]{1,0:T(8,128)S(1)}) all-reduce(f32[8,256]{1,0:T(8,128)S(1)} %get-tuple-element.6, f32[8,256]{1,0:T(8,128)S(1)} %get-tuple-element.5), channel_id=1, replica_groups=mesh['dp'=4,'tensor'=8] {'tensor'}, use_global_device_ids=true, to_apply=%region_3.0 | all-reduce | flops 4096 | bytes 32768 | tf_op jit(solution)/shard_map/psum | solution.py:110
  38.9 2.0 fusion.54
  42.9 2.2 multiply_convert_fusion.4
  45.6 5.4 %collective-permute-done.7 = f32[16,3,144]{2,0,1:T(8,128)S(1)} collective-permute-done((f32[16,3,144]{2,0,1:T(8,128)S(1)}, f32[16,3,144]{2,0,1:T(8,128)S(1)}, u32[]{:S(2)}, u32[]{:S(2)}) %collective-permute-start.7) | collective-permute-done | bytes 27680 | tf_op jit(solution)/shard_map/ppermute | solution.py:71
  51.0 6.5 %collective-permute-done.8 = f32[16,3,144]{2,0,1:T(8,128)S(1)} collective-permute-done((f32[16,3,144]{2,0,1:T(8,128)S(1)}, f32[16,3,144]{2,0,1:T(8,128)S(1)}, u32[]{:S(2)}, u32[]{:S(2)}) %collective-permute-start.8) | collective-permute-done | bytes 27680 | tf_op jit(solution)/shard_map/ppermute | solution.py:71
  57.5 6.5 %collective-permute-done.9 = f32[16,3,144]{2,0,1:T(8,128)S(1)} collective-permute-done((f32[16,3,144]{2,0,1:T(8,128)S(1)}, f32[16,3,144]{2,0,1:T(8,128)S(1)}, u32[]{:S(2)}, u32[]{:S(2)}) %collective-permute-start.9) | collective-permute-done | bytes 27680 | tf_op jit(solution)/shard_map/ppermute | solution.py:71
  64.1 6.5 %collective-permute-done.10 = f32[16,3,144]{2,0,1:T(8,128)S(1)} collective-permute-done((f32[16,3,144]{2,0,1:T(8,128)S(1)}, f32[16,3,144]{2,0,1:T(8,128)S(1)}, u32[]{:S(2)}, u32[]{:S(2)}) %collective-permute-start.10) | collective-permute-done | bytes 27680 | tf_op jit(solution)/shard_map/ppermute | solution.py:71
  70.6 6.5 %collective-permute-done.11 = f32[16,3,144]{2,0,1:T(8,128)S(1)} collective-permute-done((f32[16,3,144]{2,0,1:T(8,128)S(1)}, f32[16,3,144]{2,0,1:T(8,128)S(1)}, u32[]{:S(2)}, u32[]{:S(2)}) %collective-permute-start.11) | collective-permute-done | bytes 27680 | tf_op jit(solution)/shard_map/ppermute | solution.py:71
  77.1 6.5 %collective-permute-done.12 = f32[16,3,144]{2,0,1:T(8,128)S(1)} collective-permute-done((f32[16,3,144]{2,0,1:T(8,128)S(1)}, f32[16,3,144]{2,0,1:T(8,128)S(1)}, u32[]{:S(2)}, u32[]{:S(2)}) %collective-permute-start.12) | collective-permute-done | bytes 27680 | tf_op jit(solution)/shard_map/ppermute | solution.py:71
  83.6 6.5 %collective-permute-done.13 = f32[16,3,144]{2,0,1:T(8,128)S(1)} collective-permute-done((f32[16,3,144]{2,0,1:T(8,128)S(1)}, f32[16,3,144]{2,0,1:T(8,128)S(1)}, u32[]{:S(2)}, u32[]{:S(2)}) %collective-permute-start.13) | collective-permute-done | bytes 27680 | tf_op jit(solution)/shard_map/ppermute | solution.py:71
  90.5 3.4 all-gather.3.cloned.1.call-done
  93.8 10.8 %fusion.31 = bf16[16,256,432]{1,2,0:T(8,128)(2,1)S(1)} fusion(bf16[8,256,1152]{1,2,0:T(8,128)(2,1)} %all-gather.3.cloned.1.call-done, f32[16,1152]{1,0:T(8,128)S(1)} %get-tuple-element.12, f32[16,1152]{1,0:T(8,128)S(1)} %get-tuple-element.11, bf16[1152,432]{0,1:T(8,128)(2,1)S(1)} %copy-done.12), kind=kOutput, calls=%fused_computation.35 | convolution fusion | flops 4111663104 | bytes 9400320 | tf_op jit(solution)/shard_map/bld,df->blf/dot_general | solution.py:78
  104.6 1.7 copy-done.6
  107.6 6.3 %fusion.96 = (f32[16,2,256]{2,1,0:T(2,128)S(1)}, f32[16,2,256,256]{2,3,1,0:T(8,128)S(1)}) fusion(f32[16,2,256,256]{2,3,1,0:T(8,128)S(1)} %fusion.59), kind=kOutput, calls=%fused_computation.136 | output fusion | flops 8388863 | bytes 16809984 | tf_op jit(solution)/shard_map/sub | solution.py:29
  114.0 2.3 fusion.37
  116.3 5.3 %convolution_convert_fusion = bf16[16,256,1152]{1,2,0:T(8,128)(2,1)} fusion(bf16[16,256,144]{1,2,0:T(8,128)(2,1)S(1)} %bitcast.140, bf16[144,1152]{1,0:T(8,128)(2,1)S(1)} %copy-done.10), kind=kOutput, calls=%fused_computation.4 | convolution fusion | flops 1363673088 | bytes 10948608 | tf_op jit(solution)/shard_map/blf,fd->bld/dot_general | solution.py:80
  123.5 4.8 collective-permute-done
  128.3 5.7 %collective-permute-done.1 = f32[8,3,144]{2,0,1:T(8,128)S(1)} collective-permute-done((f32[8,3,144]{2,0,1:T(8,128)S(1)}, f32[8,3,144]{2,0,1:T(8,128)S(1)}, u32[]{:S(2)}, u32[]{:S(2)}) %collective-permute-start.1) | collective-permute-done | bytes 13856 | tf_op jit(solution)/shard_map/ppermute | solution.py:71
  134.0 5.7 %collective-permute-done.2 = f32[8,3,144]{2,0,1:T(8,128)S(1)} collective-permute-done((f32[8,3,144]{2,0,1:T(8,128)S(1)}, f32[8,3,144]{2,0,1:T(8,128)S(1)}, u32[]{:S(2)}, u32[]{:S(2)}) %collective-permute-start.2) | collective-permute-done | bytes 13856 | tf_op jit(solution)/shard_map/ppermute | solution.py:71
  139.7 5.7 %collective-permute-done.3 = f32[8,3,144]{2,0,1:T(8,128)S(1)} collective-permute-done((f32[8,3,144]{2,0,1:T(8,128)S(1)}, f32[8,3,144]{2,0,1:T(8,128)S(1)}, u32[]{:S(2)}, u32[]{:S(2)}) %collective-permute-start.3) | collective-permute-done | bytes 13856 | tf_op jit(solution)/shard_map/ppermute | solution.py:71
  145.4 5.7 %collective-permute-done.4 = f32[8,3,144]{2,0,1:T(8,128)S(1)} collective-permute-done((f32[8,3,144]{2,0,1:T(8,128)S(1)}, f32[8,3,144]{2,0,1:T(8,128)S(1)}, u32[]{:S(2)}, u32[]{:S(2)}) %collective-permute-start.4) | collective-permute-done | bytes 13856 | tf_op jit(solution)/shard_map/ppermute | solution.py:71
  151.1 5.7 %collective-permute-done.5 = f32[8,3,144]{2,0,1:T(8,128)S(1)} collective-permute-done((f32[8,3,144]{2,0,1:T(8,128)S(1)}, f32[8,3,144]{2,0,1:T(8,128)S(1)}, u32[]{:S(2)}, u32[]{:S(2)}) %collective-permute-start.5) | collective-permute-done | bytes 13856 | tf_op jit(solution)/shard_map/ppermute | solution.py:71
  156.8 5.7 %collective-permute-done.6 = f32[8,3,144]{2,0,1:T(8,128)S(1)} collective-permute-done((f32[8,3,144]{2,0,1:T(8,128)S(1)}, f32[8,3,144]{2,0,1:T(8,128)S(1)}, u32[]{:S(2)}, u32[]{:S(2)}) %collective-permute-start.6) | collective-permute-done | bytes 13856 | tf_op jit(solution)/shard_map/ppermute | solution.py:71
  162.8 5.9 %fusion.36 = bf16[8,256,432]{1,2,0:T(8,128)(2,1)S(1)} fusion(bf16[8,256,1152]{1,2,0:T(8,128)(2,1)} %all-gather.3.cloned.1.call-done, f32[8,1152]{1,0:T(8,128)S(1)} %get-tuple-element.14, f32[8,1152]{1,0:T(8,128)S(1)} %get-tuple-element.13, bf16[1152,432]{0,1:T(8,128)(2,1)S(1)} %copy-done.13), kind=kOutput, calls=%fused_computation.50 | convolution fusion | flops 2048753664 | bytes 7557120 | tf_op jit(solution)/shard_map/bld,df->blf/dot_general | solution.py:78
  169.4 3.2 fusion.95
  174.7 3.6 convolution_convert_fusion.2
  178.8 42.8 %reduce-scatter.13.cloned.1.call-done = bf16[16,256,144]{1,2,0:T(8,128)(2,1)} async-done(((bf16[16,256,1152]{1,2,0:T(8,128)(2,1)}), bf16[16,256,144]{1,2,0:T(8,128)(2,1)}) %reduce-scatter.13.cloned.1.call-update) | async-done | bytes 1179664 | tf_op jit(solution)/shard_map/reduce_scatter | solution.py:83
  221.6 3.0 fusion.57
  224.7 52.3 %reduce-scatter.11.cloned.1.call-done = bf16[8,256,144]{1,2,0:T(8,128)(2,1)} async-done(((bf16[8,256,1152]{1,2,0:T(8,128)(2,1)}), bf16[8,256,144]{1,2,0:T(8,128)(2,1)}) %reduce-scatter.11.cloned.1.call-update) | async-done | bytes 589840 | tf_op jit(solution)/shard_map/reduce_scatter | solution.py:83
  277.0 2.7 fusion.51
  280.8 49.8 %all-gather.5.cloned.1.call-done = bf16[8,256,1152]{1,2,0:T(8,128)(2,1)} async-done(((bf16[8,256,144]{1,2,0:T(8,128)(2,1)}), bf16[8,256,1152]{1,2,0:T(8,128)(2,1)}) %all-gather.5.cloned.1.call-update) | async-done | bytes 4718608 | tf_op jit(solution)/shard_map/all_gather | solution.py:146
  330.6 3.3 convolution_convert_fusion.4
  333.8 3.9 fusion.66
  337.7 7.6 %fusion.48 = bf16[8,256,2,1,72]{1,4,2,0,3:T(8,128)(2,1)S(1)} fusion(f32[8,2,256,256]{2,3,1,0:T(8,128)} %fusion.66, bf16[8,256,2,3,72]{1,4,3,2,0:T(8,128)(2,1)} %bitcast.136, f32[8,2,256,256]{2,3,1,0:T(8,128)} %copy-done.3, f32[8,2,256]{2,1,0:T(2,128)S(1)} %get-tuple-element.17), kind=kOutput, calls=%fused_computation.63 | convolution fusion | flops 158634240 | bytes 17989632 | tf_op jit(solution)/shard_map/bhlm,bmhe->blhe/dot_general | solution.py:49
  345.3 7.7 %fusion.45 = bf16[8,256,2,1,72]{1,4,2,0,3:T(8,128)(2,1)S(1)} fusion(f32[8,2,256,256]{2,3,1,0:T(8,128)} %fusion.66, bf16[8,256,2,3,72]{1,4,3,2,0:T(8,128)(2,1)} %bitcast.137, f32[8,2,256,256]{2,3,1,0:T(8,128)} %copy-done.3, f32[8,2,256]{2,1,0:T(2,128)S(1)} %get-tuple-element.17), kind=kOutput, calls=%fused_computation.62 | convolution fusion | flops 158634240 | bytes 17989632 | tf_op jit(solution)/shard_map/bhlm,blhe->bmhe/dot_general | solution.py:52
  353.0 3.0 fusion.44
  357.5 4.4 convolution_convert_fusion.1
  362.0 4.0 fusion.32
  367.1 6.4 %fusion.23 = bf16[1152,432]{1,0:T(8,128)(2,1)} fusion(bf16[8,256,432]{1,2,0:T(8,128)(2,1)} %bitcast.132, bf16[8,256,1152]{1,2,0:T(8,128)(2,1)} %all-gather.3.cloned.1.call-done, f32[8,1152]{1,0:T(8,128)S(1)} %get-tuple-element.14, f32[8,1152]{1,0:T(8,128)S(1)} %get-tuple-element.13), kind=kOutput, calls=%fused_computation.29 | convolution fusion | flops 2048366592 | bytes 7557120 | tf_op jit(solution)/shard_map/bld,blf->df/dot_general | solution.py:154
  373.8 42.0 %reduce-scatter.17.cloned.1.call-done = bf16[8,256,144]{1,2,0:T(8,128)(2,1)} async-done(((bf16[8,256,1152]{1,2,0:T(8,128)(2,1)}), bf16[8,256,144]{1,2,0:T(8,128)(2,1)}) %reduce-scatter.17.cloned.1.call-update) | async-done | bytes 589840 | tf_op jit(solution)/shard_map/reduce_scatter | solution.py:160
  415.8 1.7 convert_reduce_fusion.1
  418.5 3.2 copy.81
  421.7 5.5 %reshape.56 = bf16[1152,432]{1,0:T(8,128)(2,1)} reshape(bf16[1152,3,144]{2,1,0:T(4,128)(2,1)} %bitcast.124) | data formatting | bytes 1990656
  427.2 15.7 %reduce-scatter.19.cloned.1.call-done = bf16[288,144]{1,0:T(8,128)(2,1)} async-done(((bf16[1152,144]{1,0:T(8,128)(2,1)}), bf16[288,144]{1,0:T(8,128)(2,1)}) %reduce-scatter.19.cloned.1.call-update) | async-done | bytes 82960
  444.7 29.9 %reduce-scatter.15.cloned.1.call-done = bf16[288,432]{1,0:T(8,128)(2,1)} async-done(((bf16[1152,432]{1,0:T(8,128)(2,1)}), bf16[288,432]{1,0:T(8,128)(2,1)}) %reduce-scatter.15.cloned.1.call-update) | async-done | bytes 248848 | tf_op jit(solution)/shard_map/reduce_scatter | solution.py:173
  474.6 1.8 convert_element_type.147
  476.5 29.8 %reduce-scatter.21.cloned.1.call-done = bf16[288,432]{1,0:T(8,128)(2,1)} async-done(((bf16[1152,432]{1,0:T(8,128)(2,1)}), bf16[288,432]{1,0:T(8,128)(2,1)}) %reduce-scatter.21.cloned.1.call-update) | async-done | bytes 248848
  506.3 1.8 reshape.57
  (93 shorter events, 19.0 us)
Async XLA Ops:
  7.2 34.6 %copy-start = (bf16[1000,1152]{1,0:T(8,128)(2,1)S(1)}, bf16[1000,1152]{1,0:T(8,128)(2,1)}, u32[]{:S(2)}) copy-start(bf16[1000,1152]{1,0:T(8,128)(2,1)} %param.19) | copy-start | bytes 6912004
  7.2 35.8 %copy-start.11 = (s32[8]{0:T(128)S(1)}, s32[8]{0:T(128)}, u32[]{:S(2)}) copy-start(s32[8]{0:T(128)} %param.15) | copy-start | bytes 100
  7.2 38.0 %copy-start.8 = (bf16[3,1152,144]{1,2,0:T(8,128)(2,1)S(1)}, bf16[3,1152,144]{1,2,0:T(8,128)(2,1)}, u32[]{:S(2)}) copy-start(bf16[3,1152,144]{1,2,0:T(8,128)(2,1)} %param.24) | copy-start | bytes 2985988
  7.2 86.6 %all-gather.3.cloned.1.call-start = ((), (), s32[]{:S(2)}) async-start(), calls=%async_computation.6 | async-start | bytes 5308416 | tf_op jit(solution)/shard_map/all_gather | solution.py:129
  41.0 180.6 %reduce-scatter.13.cloned.1.call-start = ((), (), s32[]{:S(2)}) async-start(), calls=%async_computation.8 | async-start | bytes 10616832 | tf_op jit(solution)/shard_map/reduce_scatter | solution.py:83
  42.9 50.9 %copy-start.12 = (bf16[1152,432]{0,1:T(8,128)(2,1)S(1)}, bf16[1152,432]{0,1:T(8,128)(2,1)}, u32[]{:S(2)}) copy-start(bf16[1152,432]{0,1:T(8,128)(2,1)} %param.22) | copy-start | bytes 2985988
  45.6 5.4 %collective-permute-start.7 = (f32[16,3,144]{2,0,1:T(8,128)S(1)}, f32[16,3,144]{2,0,1:T(8,128)S(1)}, u32[]{:S(2)}, u32[]{:S(2)}) collective-permute-start(f32[16,3,144]{2,0,1:T(8,128)S(1)} %fusion.72), channel_id=1, source_target_pairs={{0,1},{1,2},{2,3},{3,4},{4,5},{5,6},{6,7},{7,0},{8,9},{9,10},{10,1... | collective-permute-start | bytes 82952 | tf_op jit(solution)/shard_map/ppermute | solution.py:71
  51.0 6.5 %collective-permute-start.8 = (f32[16,3,144]{2,0,1:T(8,128)S(1)}, f32[16,3,144]{2,0,1:T(8,128)S(1)}, u32[]{:S(2)}, u32[]{:S(2)}) collective-permute-start(f32[16,3,144]{2,0,1:T(8,128)S(1)} %collective-permute-done.7), channel_id=1, source_target_pairs={{0,1},{1,2},{2,3},{3,4},{4,5},{5,6},{6,7},{7,0},{8,9},{9,10},{10,1... | collective-permute-start | bytes 82952 | tf_op jit(solution)/shard_map/ppermute | solution.py:71
  57.5 6.5 %collective-permute-start.9 = (f32[16,3,144]{2,0,1:T(8,128)S(1)}, f32[16,3,144]{2,0,1:T(8,128)S(1)}, u32[]{:S(2)}, u32[]{:S(2)}) collective-permute-start(f32[16,3,144]{2,0,1:T(8,128)S(1)} %collective-permute-done.8), channel_id=1, source_target_pairs={{0,1},{1,2},{2,3},{3,4},{4,5},{5,6},{6,7},{7,0},{8,9},{9,10},{10,1... | collective-permute-start | bytes 82952 | tf_op jit(solution)/shard_map/ppermute | solution.py:71
  64.0 6.5 %collective-permute-start.10 = (f32[16,3,144]{2,0,1:T(8,128)S(1)}, f32[16,3,144]{2,0,1:T(8,128)S(1)}, u32[]{:S(2)}, u32[]{:S(2)}) collective-permute-start(f32[16,3,144]{2,0,1:T(8,128)S(1)} %collective-permute-done.9), channel_id=1, source_target_pairs={{0,1},{1,2},{2,3},{3,4},{4,5},{5,6},{6,7},{7,0},{8,9},{9,10},{10,1... | collective-permute-start | bytes 82952 | tf_op jit(solution)/shard_map/ppermute | solution.py:71
  70.6 6.5 %collective-permute-start.11 = (f32[16,3,144]{2,0,1:T(8,128)S(1)}, f32[16,3,144]{2,0,1:T(8,128)S(1)}, u32[]{:S(2)}, u32[]{:S(2)}) collective-permute-start(f32[16,3,144]{2,0,1:T(8,128)S(1)} %collective-permute-done.10), channel_id=1, source_target_pairs={{0,1},{1,2},{2,3},{3,4},{4,5},{5,6},{6,7},{7,0},{8,9},{9,10},{10,1... | collective-permute-start | bytes 82952 | tf_op jit(solution)/shard_map/ppermute | solution.py:71
  77.1 6.5 %collective-permute-start.12 = (f32[16,3,144]{2,0,1:T(8,128)S(1)}, f32[16,3,144]{2,0,1:T(8,128)S(1)}, u32[]{:S(2)}, u32[]{:S(2)}) collective-permute-start(f32[16,3,144]{2,0,1:T(8,128)S(1)} %collective-permute-done.11), channel_id=1, source_target_pairs={{0,1},{1,2},{2,3},{3,4},{4,5},{5,6},{6,7},{7,0},{8,9},{9,10},{10,1... | collective-permute-start | bytes 82952 | tf_op jit(solution)/shard_map/ppermute | solution.py:71
  83.5 6.5 %collective-permute-start.13 = (f32[16,3,144]{2,0,1:T(8,128)S(1)}, f32[16,3,144]{2,0,1:T(8,128)S(1)}, u32[]{:S(2)}, u32[]{:S(2)}) collective-permute-start(f32[16,3,144]{2,0,1:T(8,128)S(1)} %collective-permute-done.12), channel_id=1, source_target_pairs={{0,1},{1,2},{2,3},{3,4},{4,5},{5,6},{6,7},{7,0},{8,9},{9,10},{10,1... | collective-permute-start | bytes 82952 | tf_op jit(solution)/shard_map/ppermute | solution.py:71
  104.6 1.8 copy-start.6
  114.0 2.3 copy-start.10
  121.6 0.9 copy-start.15
  121.6 0.9 copy-start.16
  121.6 1.3 copy-start.9
  121.6 41.2 %copy-start.13 = (bf16[1152,432]{0,1:T(8,128)(2,1)S(1)}, bf16[1152,432]{0,1:T(8,128)(2,1)}, u32[]{:S(2)}) copy-start(bf16[1152,432]{0,1:T(8,128)(2,1)} %param.25) | copy-start | bytes 2985988
  121.6 155.3 %reduce-scatter.11.cloned.1.call-start = ((), (), s32[]{:S(2)}) async-start(), calls=%async_computation.7 | async-start | bytes 5308416 | tf_op jit(solution)/shard_map/reduce_scatter | solution.py:83
  123.3 5.0 collective-permute-start
  128.3 5.7 %collective-permute-start.1 = (f32[8,3,144]{2,0,1:T(8,128)S(1)}, f32[8,3,144]{2,0,1:T(8,128)S(1)}, u32[]{:S(2)}, u32[]{:S(2)}) collective-permute-start(f32[8,3,144]{2,0,1:T(8,128)S(1)} %collective-permute-done), channel_id=1, source_target_pairs={{0,1},{1,2},{2,3},{3,4},{4,5},{5,6},{6,7},{7,0},{8,9},{9,10},{10,1... | collective-permute-start | bytes 41480 | tf_op jit(solution)/shard_map/ppermute | solution.py:71
  134.0 5.7 %collective-permute-start.2 = (f32[8,3,144]{2,0,1:T(8,128)S(1)}, f32[8,3,144]{2,0,1:T(8,128)S(1)}, u32[]{:S(2)}, u32[]{:S(2)}) collective-permute-start(f32[8,3,144]{2,0,1:T(8,128)S(1)} %collective-permute-done.1), channel_id=1, source_target_pairs={{0,1},{1,2},{2,3},{3,4},{4,5},{5,6},{6,7},{7,0},{8,9},{9,10},{10,1... | collective-permute-start | bytes 41480 | tf_op jit(solution)/shard_map/ppermute | solution.py:71
  139.7 5.7 %collective-permute-start.3 = (f32[8,3,144]{2,0,1:T(8,128)S(1)}, f32[8,3,144]{2,0,1:T(8,128)S(1)}, u32[]{:S(2)}, u32[]{:S(2)}) collective-permute-start(f32[8,3,144]{2,0,1:T(8,128)S(1)} %collective-permute-done.2), channel_id=1, source_target_pairs={{0,1},{1,2},{2,3},{3,4},{4,5},{5,6},{6,7},{7,0},{8,9},{9,10},{10,1... | collective-permute-start | bytes 41480 | tf_op jit(solution)/shard_map/ppermute | solution.py:71
  145.4 5.7 %collective-permute-start.4 = (f32[8,3,144]{2,0,1:T(8,128)S(1)}, f32[8,3,144]{2,0,1:T(8,128)S(1)}, u32[]{:S(2)}, u32[]{:S(2)}) collective-permute-start(f32[8,3,144]{2,0,1:T(8,128)S(1)} %collective-permute-done.3), channel_id=1, source_target_pairs={{0,1},{1,2},{2,3},{3,4},{4,5},{5,6},{6,7},{7,0},{8,9},{9,10},{10,1... | collective-permute-start | bytes 41480 | tf_op jit(solution)/shard_map/ppermute | solution.py:71
  151.1 5.7 %collective-permute-start.5 = (f32[8,3,144]{2,0,1:T(8,128)S(1)}, f32[8,3,144]{2,0,1:T(8,128)S(1)}, u32[]{:S(2)}, u32[]{:S(2)}) collective-permute-start(f32[8,3,144]{2,0,1:T(8,128)S(1)} %collective-permute-done.4), channel_id=1, source_target_pairs={{0,1},{1,2},{2,3},{3,4},{4,5},{5,6},{6,7},{7,0},{8,9},{9,10},{10,1... | collective-permute-start | bytes 41480 | tf_op jit(solution)/shard_map/ppermute | solution.py:71
  156.8 5.7 %collective-permute-start.6 = (f32[8,3,144]{2,0,1:T(8,128)S(1)}, f32[8,3,144]{2,0,1:T(8,128)S(1)}, u32[]{:S(2)}, u32[]{:S(2)}) collective-permute-start(f32[8,3,144]{2,0,1:T(8,128)S(1)} %collective-permute-done.5), channel_id=1, source_target_pairs={{0,1},{1,2},{2,3},{3,4},{4,5},{5,6},{6,7},{7,0},{8,9},{9,10},{10,1... | collective-permute-start | bytes 41480 | tf_op jit(solution)/shard_map/ppermute | solution.py:71
  168.6 4.0 copy-start.5
  172.7 2.0 copy-start.3
  172.7 2.0 copy-start.7
  174.7 3.9 copy-start.17
  178.3 98.7 %copy-start.2 = (bf16[8,256,144]{1,2,0:T(8,128)(2,1)S(1)}, bf16[8,256,144]{1,2,0:T(8,128)(2,1)}, u32[]{:S(2)}) copy-start(bf16[8,256,144]{1,2,0:T(8,128)(2,1)} %param.14) | copy-start | bytes 1769476
  178.4 152.2 %all-gather.5.cloned.1.call-start = ((), (), s32[]{:S(2)}) async-start(), calls=%async_computation.9 | async-start | bytes 5308416 | tf_op jit(solution)/shard_map/all_gather | solution.py:146
  280.7 135.0 %reduce-scatter.17.cloned.1.call-start = ((), (), s32[]{:S(2)}) async-start(), calls=%async_computation.11 | async-start | bytes 5308416 | tf_op jit(solution)/shard_map/reduce_scatter | solution.py:160
  356.0 1.5 copy-start.14
  356.3 1.2 copy-start.4
  362.0 81.0 %reduce-scatter.19.cloned.1.call-start = ((), (), s32[]{:S(2)}) async-start(), calls=%async_computation.12 | async-start | bytes 737280
  367.1 107.5 %reduce-scatter.15.cloned.1.call-start = ((), (), s32[]{:S(2)}) async-start(), calls=%async_computation.10 | async-start | bytes 1474560 | tf_op jit(solution)/shard_map/reduce_scatter | solution.py:173
  373.5 132.7 %reduce-scatter.21.cloned.1.call-start = ((), (), s32[]{:S(2)}) async-start(), calls=%async_computation.13 | async-start | bytes 1474560
  421.7 87.7 %copy-start.1 = (bf16[1000,1152]{1,0:T(8,128)(2,1)S(1)}, bf16[1000,1152]{1,0:T(8,128)(2,1)}, u32[]{:S(2)}) copy-start(bf16[1000,1152]{1,0:T(8,128)(2,1)} %param.19) | copy-start | bytes 6912004
Sparse Core Ops, SparseCore 0:
  41.1 52.6 all-gather.2
  121.8 99.7 reduce-scatter.12
  223.9 53.0 reduce-scatter.10
  280.9 49.6 all-gather.4
  362.1 53.6 reduce-scatter.16
  419.1 23.8 reduce-scatter.18
  445.9 28.6 reduce-scatter.14
  477.5 28.6 reduce-scatter.20
